TPU v7x, 32 devices: a whole 2x2x4 slice. The times are simulated.
32 devices in a mesh: rows: 4 (over x, core), batch: 8 (over z, y).
Axes of the slice: x: 2, y: 2, z: 4, core: 2. Of those that a mesh axis runs over, the one named last changes fastest.
Arguments:
- features: bfloat16 [96, 8, 32, 512], P('batch', 'rows'), may hold values from -12 to 12
- norm_gain: float32 [512], replicated, may hold values from 0.25 to 1.75
- norm_bias: float32 [512], replicated, may hold values from -2.5 to 2.5
- conv_weight: bfloat16 [4, 4608], replicated, may hold values from -0.09375 to 0.09375
- embed_weight: float32 [16, 1024], replicated, may hold values from -1.5 to 1.5
- embed_bias: float32 [1024], replicated, may hold values from -2.5 to 2.5
- proj_in: bfloat16 [1024, 2048], P('rows'), may hold values from -0.1875 to 0.1875
- proj_in_bias: float32 [2048], replicated, may hold values from -2.5 to 2.5
- proj_out: bfloat16 [2048, 768], P('rows'), may hold values from -0.125 to 0.125
- proj_out_bias: float32 [768], replicated, may hold values from -2.5 to 2.5
- targets: bfloat16 [96, 4, 16, 768], P('batch', 'rows'), may hold values from -6 to 6
Outputs:
- grad_features: bfloat16 [96, 8, 32, 512], P('batch', 'rows')
- grad_conv: float32 [4, 4608], replicated
- grad_gain: float32 [512], replicated
- grad_bias: float32 [512], replicated
- grad_embed: float32 [16, 1024], replicated
All inputs are finite; a program needn't handle non-finite values.
Results may differ from a plain program's by a relative error of at most 0.012.
Values may be sent and summed in bfloat16 or wider, within the bound.
A program may use at most 128 MiB of HBM per device.

v0:
```python
import jax
import jax.numpy as jnp
from jax import lax
from jax.sharding import PartitionSpec as P

GROUPS = 32
LATENT = 4
PATCH = 2
ALIGN = 768


EPS_NORM = 1e-06
EPS_UNIT = 1e-06


def padded(block, sides, width):
    for axis, dim in sides:
        count = lax.axis_size(axis)
        forward = [(i, i + 1) for i in range(count - 1)]
        backward = [(target, source) for source, target in forward]
        low = lax.ppermute(
            lax.slice_in_dim(block, block.shape[dim] - width, None, axis=dim), axis, forward
        )
        high = lax.ppermute(lax.slice_in_dim(block, 0, width, axis=dim), axis, backward)
        block = jnp.concatenate([low, block, high], axis=dim)
    return block


def swish_slope(values):
    sig = jax.nn.sigmoid(values)
    return sig * (1.0 + values * (1.0 - sig))


def shards(
    features,
    norm_gain,
    norm_bias,
    conv_weight,
    embed_weight,
    embed_bias,
    proj_in,
    proj_in_bias,
    proj_out,
    proj_out_bias,
    targets,
):
    images, height, across, channels = features.shape
    per_group = channels // GROUPS
    members = lax.axis_size("rows") * height * across * per_group
    cell_count = images * height * across
    values = features.astype(jnp.float32)
    grouped = values.reshape(images, height * across, GROUPS, per_group)
    totals = lax.psum(jnp.sum(grouped, axis=(1, 3)), "rows")
    centred = grouped - (totals / members)[:, None, :, None]
    squares = lax.psum(jnp.sum(centred * centred, axis=(1, 3)), "rows")
    variance = squares / members
    inverse = lax.rsqrt(variance + EPS_NORM)[:, None, :, None]
    normed = (centred * inverse).reshape(images, height, across, channels)
    shifted = normed * norm_gain + norm_bias
    active = (shifted * jax.nn.sigmoid(shifted)).astype(jnp.bfloat16)
    active_flat = active.reshape(cell_count, channels)
    kernel_stack = (
        conv_weight.reshape(LATENT, 9, channels).transpose(2, 1, 0).reshape(channels, 9 * LATENT)
    )
    tap_terms = jnp.dot(active_flat, kernel_stack, preferred_element_type=jnp.float32)
    tap_terms = tap_terms.reshape(images, height, across, 9, LATENT)
    tap_pad = jnp.pad(tap_terms, ((0, 0), (2, 2), (1, 1), (0, 0), (0, 0)))
    extended = jnp.zeros((images, height + 2, across, LATENT), jnp.float32)
    for position in range(9):
        row_off, col_off = (position // 3, position % 3)
        extended = (
            extended
            + tap_pad[:, row_off : row_off + height + 2, col_off : col_off + across, position, :]
        )
    edges = jnp.concatenate([extended[:, 0:1], extended[:, height + 1 : height + 2]], axis=1)
    arrived = padded(edges, (("rows", 1),), 1)
    latent = extended[:, 1 : height + 1]
    latent = latent.at[:, 0].add(arrived[:, 0])
    latent = latent.at[:, height - 1].add(arrived[:, 3])
    tok_rows = height // PATCH
    tok_cols = across // PATCH
    tok_count = images * tok_rows * tok_cols
    patches = (
        latent.reshape(images, tok_rows, PATCH, tok_cols, PATCH, LATENT)
        .transpose(0, 1, 3, 2, 4, 5)
        .reshape(tok_count, PATCH * PATCH * LATENT)
    )
    embedded = (
        jnp.dot(patches, embed_weight, precision=lax.Precision.HIGHEST) + embed_bias
    ).astype(jnp.bfloat16)
    full_in, full_out = (
        lax.all_gather(proj_in, "rows", axis=0, tiled=True),
        lax.all_gather(proj_out, "rows", axis=0, tiled=True),
    )
    hidden_pre = jnp.dot(embedded, full_in, preferred_element_type=jnp.float32) + proj_in_bias
    hidden_act = (hidden_pre * jax.nn.sigmoid(hidden_pre)).astype(jnp.bfloat16)
    projected = jnp.dot(hidden_act, full_out, preferred_element_type=jnp.float32) + proj_out_bias
    target = targets.reshape(tok_count, ALIGN).astype(jnp.float32)
    unit_target = target * lax.rsqrt(jnp.sum(target * target, axis=1, keepdims=True) + EPS_UNIT)
    inv_len = lax.rsqrt(jnp.sum(projected * projected, axis=1, keepdims=True) + EPS_UNIT)
    unit_proj = projected * inv_len
    cosine = jnp.sum(unit_proj * unit_target, axis=1, keepdims=True)
    grad_out = (-inv_len * (unit_target - cosine * unit_proj)).astype(jnp.bfloat16)
    back_hidden = lax.dot_general(
        grad_out, full_out, (((1,), (1,)), ((), ())), preferred_element_type=jnp.float32
    )
    grad_hidden = (back_hidden * swish_slope(hidden_pre)).astype(jnp.bfloat16)
    grad_embedded = lax.dot_general(
        grad_hidden, full_in, (((1,), (1,)), ((), ())), preferred_element_type=jnp.float32
    )
    embed_part = lax.dot_general(
        patches, grad_embedded, (((0,), (0,)), ((), ())), precision=lax.Precision.HIGHEST
    )
    grad_patch = lax.dot_general(
        grad_embedded, embed_weight, (((1,), (1,)), ((), ())), precision=lax.Precision.HIGHEST
    )
    grad_latent = (
        grad_patch.reshape(images, tok_rows, tok_cols, PATCH, PATCH, LATENT)
        .transpose(0, 1, 3, 2, 4, 5)
        .reshape(images, height, across, LATENT)
        .astype(jnp.bfloat16)
    )
    grad_pad = padded(grad_latent, (("rows", 1),), 1)
    grad_pad = jnp.pad(grad_pad, ((0, 0), (0, 0), (1, 1), (0, 0)))
    shifted_grads = []
    for position in range(9):
        row_off, col_off = (position // 3, position % 3)
        shifted_grads.append(
            grad_pad[:, 2 - row_off : 2 - row_off + height, 2 - col_off : 2 - col_off + across, :]
        )
    grad_taps = jnp.concatenate(shifted_grads, axis=3).reshape(cell_count, 9 * LATENT)
    conv_stack = lax.dot_general(
        active_flat, grad_taps, (((0,), (0,)), ((), ())), preferred_element_type=jnp.float32
    )
    conv_part = (
        conv_stack.reshape(channels, 9, LATENT).transpose(2, 1, 0).reshape(LATENT, 9 * channels)
    )
    grad_active = lax.dot_general(
        grad_taps, kernel_stack, (((1,), (1,)), ((), ())), preferred_element_type=jnp.float32
    )
    flat_shift = shifted.reshape(cell_count, channels)
    flat_normed = normed.reshape(cell_count, channels)
    grad_shift = grad_active * swish_slope(flat_shift)
    gain_part = jnp.sum(grad_shift * flat_normed, axis=0)
    bias_part = jnp.sum(grad_shift, axis=0)
    grad_norm = (grad_shift * norm_gain).reshape(images, height * across, GROUPS, per_group)
    normed_groups = flat_normed.reshape(images, height * across, GROUPS, per_group)
    first, second = lax.psum(
        (jnp.sum(grad_norm, axis=(1, 3)), jnp.sum(grad_norm * normed_groups, axis=(1, 3))), "rows"
    )
    grad_values = inverse * (
        grad_norm
        - (first / members)[:, None, :, None]
        - normed_groups * (second / members)[:, None, :, None]
    )
    grad_features = grad_values.reshape(images, height, across, channels).astype(jnp.bfloat16)
    grad_conv, grad_gain, grad_bias, grad_embed = lax.psum(
        (conv_part, gain_part, bias_part, embed_part), ("rows", "batch")
    )
    return (grad_features, grad_conv, grad_gain, grad_bias, grad_embed)


def solution(mesh):
    in_specs = (
        P("batch", "rows", None, None),
        P(),
        P(),
        P(),
        P(),
        P(),
        P("rows", None),
        P(),
        P("rows", None),
        P(),
        P("batch", "rows", None, None),
    )
    out_specs = (P("batch", "rows", None, None), P(), P(), P(), P())
    return jax.shard_map(shards, mesh=mesh, in_specs=in_specs, out_specs=out_specs, check_vma=False)
```

profile of v0, /device:TPU:0, one launch (start us, length us, event | category | flops | bytes accessed | tf_op | source)
XLA Modules:
  0.0 262.6 jit_solution(803283353714649149)
XLA Ops:
  9.3 8.5 %psum.56 = f32[12,32]{1,0:T(8,128)S(1)} all-reduce(f32[12,32]{1,0:T(8,128)S(1)} %reduce_sum.97), channel_id=1, replica_groups=mesh['rows'=4,'batch'=8] {'rows'}, use_global_device_ids=true, to_apply=%region_2.0 | all-reduce | flops 384 | bytes 3072 | tf_op jit(solution)/shard_map/psum | solution.py:53
  18.6 6.5 %psum.57 = f32[12,32]{1,0:T(8,128)S(1)} all-reduce(f32[12,32]{1,0:T(8,128)S(1)} %reduce_sum.100), channel_id=1, replica_groups=mesh['rows'=4,'batch'=8] {'rows'}, use_global_device_ids=true, to_apply=%region_5.6 | all-reduce | flops 384 | bytes 3072 | tf_op jit(solution)/shard_map/psum | solution.py:55
  25.3 1.7 multiply_convert_fusion.2
  30.4 3.6 %collective-permute-start = (f32[12,1,32,4]{2,3,1,0:T(4,128)}, f32[12,1,32,4]{2,3,1,0:T(4,128)}, u32[]{:S(2)}, u32[]{:S(2)}) collective-permute-start(f32[12,1,32,4]{2,3,1,0:T(4,128)} %get-tuple-element.43), channel_id=1, source_target_pairs={{0,8},{8,16},{16,24},{1,9},{9,17},{17,25},{2,10},{10,18},{18,26},{... | collective-permute-start | bytes 18440 | tf_op jit(solution)/shard_map/ppermute | solution.py:21
  35.4 6.2 %copy.155 = f32[12,2,32,512]{2,1,0,3:T(2,128)} copy(bf16[12,2,32,512]{3,2,1,0:T(8,128)(2,1)S(1)} %copy-done.1) | data formatting | bytes 2359296 | tf_op jit(solution)/shard_map/reshape | solution.py:52
  41.6 2.4 mul.163
  44.0 3.4 %mul.171 = f32[768,512]{0,1:T(8,128)S(1)} reshape(f32[12,64,32,16]{1,0,3,2:T(8,128)} %mul.163) | data formatting | bytes 3145728 | tf_op jit(solution)/shard_map/mul | solution.py:151
  47.4 1.6 copy.150
  49.1 2.4 sub.61
  51.5 3.3 %sub.64 = f32[768,512]{0,1:T(8,128)S(1)} reshape(f32[12,64,32,16]{1,0,3,2:T(8,128)} %sub.61) | data formatting | bytes 3145728 | tf_op jit(solution)/shard_map/sub | solution.py:54
  54.8 1.6 copy.149
  56.5 8.0 %reshape.201 = f32[12,64,32,16]{1,0,3,2:T(8,128)} reshape(f32[12,2,32,512]{2,1,0,3:T(2,128)} %copy.155) | data formatting | bytes 3145728 | tf_op jit(solution)/shard_map/reshape | solution.py:52
  66.6 4.3 %convolution_add_fusion = f32[192,2048]{1,0:T(8,128)} fusion(bf16[192,1024]{1,0:T(8,128)(2,1)S(1)} %fusion.10, bf16[1024,2048]{1,0:T(8,128)(2,1)} %all-gather.3.cloned.1.call-done, f32[2048]{0:T(1024)S(1)} %copy-done.6), kind=kOutput, calls=%fused_computation.11 | convolution fusion | flops 805699584 | bytes 6168576 | tf_op jit(solution)/shard_map/dot_general | solution.py:95
  70.9 6.5 %all-gather.5.cloned.1.call-done = bf16[2048,768]{1,0:T(8,128)(2,1)} async-done(((bf16[512,768]{1,0:T(8,128)(2,1)}), bf16[2048,768]{1,0:T(8,128)(2,1)}) %all-gather.5.cloned.1.call-update) | async-done | bytes 3145744 | tf_op jit(solution)/shard_map/all_gather | solution.py:93
  77.4 3.4 %multiply_reduce_fusion.4 = (f32[192]{0:T(256)S(1)}, f32[192,768]{1,0:T(8,128)S(1)}) fusion(f32[768]{0:T(1024)S(1)} %copy-done.10, bf16[2048,768]{1,0:T(8,128)(2,1)} %all-gather.5.cloned.1.call-done, f32[192,2048]{1,0:T(8,128)} %convolution_add_fusion), kind=kOutput, calls=%fused_computation.47 | convolution fusion | flops 606388032 | bytes 5312256 | tf_op jit(solution)/shard_map/dot_general | solution.py:97
  81.6 6.4 %fusion.11 = f32[192,1024]{1,0:T(8,128)S(1)} fusion(bf16[1024,2048]{1,0:T(8,128)(2,1)} %all-gather.3.cloned.1.call-done, bf16[2048,768]{1,0:T(8,128)(2,1)} %all-gather.5.cloned.1.call-done, f32[192,2048]{1,0:T(8,128)} %convolution_add_fusion, f32[192,768]{1,0:T(8,128)S(1)} %copy-done.2, f32[192,768]{1,0:T(8,128)} %copy-done.4, ...), kind=kOutput, calls=%fused_computation.37 | convolution fusion | flops 1413562368 | bytes 10881280 | tf_op jit(solution)/shard_map/dot_general | solution.py:108
  89.1 2.1 collective-permute-start.2
  102.9 3.3 %fusion.46 = (f32[512]{0:T(512)S(1)}, f32[512]{0:T(512)S(1)}, f32[768,512]{1,0:T(8,128)S(1)}) fusion(f32[768,512]{1,0:T(8,128)} %copy.150, f32[768,512]{1,0:T(8,128)} %copy.149, bf16[12,2,32,512]{3,2,1,0:T(8,128)(2,1)S(1)} %copy-done.1, f32[512]{0:T(512)S(1)} %copy-done.9, f32[12,2,32,512]{3,2,1,0:T(8,128)} %get-tuple-element.41, ...), kind=kOutput, calls=%fused_computation.94 | convolution fusion | flops 34208768 | bytes 7176192 | tf_op jit(solution)/shard_map/dot_general | solution.py:138
  106.3 1.6 copy.141
  107.9 4.0 %reshape.188 = f32[12,64,32,16]{1,0,3,2:T(8,128)} reshape(f32[768,512]{0,1:T(8,128)} %copy.141) | data formatting | bytes 3145728 | tf_op jit(solution)/shard_map/reshape | solution.py:146
  111.9 4.7 %fusion.45 = (f32[12,32]{0,1:T(8,128)S(1)}, f32[12,32]{0,1:T(8,128)S(1)}) fusion(f32[12,64,32,16]{1,0,3,2:T(8,128)} %reshape.188, f32[12,32]{0,1:T(8,128)S(1)} %copy.146, f32[12,64,32,16]{1,0,3,2:T(8,128)} %reshape.201, f32[12,32]{0,1:T(8,128)S(1)} %copy.144), kind=kLoop, calls=%fused_computation.93 | loop fusion | flops 1965312 | bytes 3151872 | tf_op jit(solution)/shard_map/reduce_sum | solution.py:149
  116.7 12.4 %all-reduce.4 = (f32[12,32]{1,0:T(8,128)S(1)}, f32[12,32]{1,0:T(8,128)S(1)}) all-reduce(f32[12,32]{1,0:T(8,128)S(1)} %copy.147, f32[12,32]{1,0:T(8,128)S(1)} %copy.142), channel_id=1, replica_groups=mesh['rows'=4,'batch'=8] {'rows'}, use_global_device_ids=true, to_apply=%region_12.13 | all-reduce | flops 768 | bytes 6144 | tf_op jit(solution)/shard_map/psum | solution.py:148
  131.0 40.5 %all-reduce.2 = (f32[512]{0:T(512)}, f32[512]{0:T(512)}) all-reduce(f32[512]{0:T(512)S(1)} %get-tuple-element.32, f32[512]{0:T(512)S(1)} %get-tuple-element.31), channel_id=1, replica_groups=mesh['rows'=4,'batch'=8] {'rows','batch'}, use_global_device_ids=true, to_apply=%region_15.16 | all-reduce | flops 1024 | bytes 8192 | tf_op jit(solution)/shard_map/psum | solution.py:157
  171.5 81.6 %all-reduce.7.cloned.1.call-done = (f32[4,4608]{1,0:T(4,128)}, f32[16,1024]{1,0:T(8,128)}) async-done(((f32[4,4608]{1,0:T(4,128)}, f32[16,1024]{1,0:T(8,128)}), (f32[4,4608]{1,0:T(4,128)}, f32[16,1024]{1,0:T(8,128)})) %all-reduce.7.cloned.1.call-update) | async-done | bytes 139280 | tf_op jit(solution)/shard_map/psum | solution.py:157
  (99 shorter events, 28.1 us)
Async XLA Ops:
  7.2 58.5 %copy-start = (f32[16,1024]{1,0:T(8,128)S(1)}, f32[16,1024]{1,0:T(8,128)}, u32[]{:S(2)}) copy-start(f32[16,1024]{1,0:T(8,128)} %param.19) | copy-start | bytes 196612
  7.2 1.6 copy-start.5
  7.2 1.7 copy-start.1
  7.2 59.4 %all-gather.3.cloned.1.call-start = ((), (), s32[]{:S(2)}) async-start(), calls=%async_computation | async-start | bytes 5242880 | tf_op jit(solution)/shard_map/all_gather | solution.py:92
  7.9 69.5 %all-gather.5.cloned.1.call-start = ((), (), s32[]{:S(2)}) async-start(), calls=%async_computation.1 | async-start | bytes 3932160 | tf_op jit(solution)/shard_map/all_gather | solution.py:93
  8.7 244.4 %all-reduce.7.cloned.1.call-start = ((), (), s32[]{:S(2)}) async-start(), calls=%async_computation.2 | async-start | bytes 278528 | tf_op jit(solution)/shard_map/psum | solution.py:157
  8.9 16.5 %copy-start.8 = (f32[512]{0:T(512)S(1)}, f32[512]{0:T(512)}, u32[]{:S(2)}) copy-start(f32[512]{0:T(512)} %param.17) | copy-start | bytes 6148
  8.9 16.5 %copy-start.9 = (f32[512]{0:T(512)S(1)}, f32[512]{0:T(512)}, u32[]{:S(2)}) copy-start(f32[512]{0:T(512)} %param.16) | copy-start | bytes 6148
  27.1 7.0 %copy-start.3 = (bf16[12,1,16,768]{3,2,1,0:T(8,128)(2,1)S(1)}, bf16[12,1,16,768]{3,2,1,0:T(8,128)(2,1)}, u32[]{:S(2)}) copy-start(bf16[12,1,16,768]{3,2,1,0:T(8,128)(2,1)} %param.25) | copy-start | bytes 884740
  29.1 36.2 %collective-permute-start.1 = (f32[12,1,32,4]{2,3,1,0:T(4,128)S(1)}, f32[12,1,32,4]{2,3,1,0:T(4,128)S(1)}, u32[]{:S(2)}, u32[]{:S(2)}) collective-permute-start(f32[12,1,32,4]{2,3,1,0:T(4,128)S(1)} %get-tuple-element.42), channel_id=1, source_target_pairs={{8,0},{16,8},{24,16},{9,1},{17,9},{25,17},{10,2},{18,10},{26,18},{... | collective-permute-start | bytes 18440 | tf_op jit(solution)/shard_map/ppermute | solution.py:24
  30.4 34.1 %collective-permute-start = (f32[12,1,32,4]{2,3,1,0:T(4,128)}, f32[12,1,32,4]{2,3,1,0:T(4,128)}, u32[]{:S(2)}, u32[]{:S(2)}) collective-permute-start(f32[12,1,32,4]{2,3,1,0:T(4,128)} %get-tuple-element.43), channel_id=1, source_target_pairs={{0,8},{8,16},{16,24},{1,9},{9,17},{17,25},{2,10},{10,18},{18,26},{... | collective-permute-start | bytes 18440 | tf_op jit(solution)/shard_map/ppermute | solution.py:21
  56.5 9.2 %copy-start.7 = (f32[1024]{0:T(1024)S(1)}, f32[1024]{0:T(1024)}, u32[]{:S(2)}) copy-start(f32[1024]{0:T(1024)} %param.20) | copy-start | bytes 12292
  56.5 10.1 %copy-start.6 = (f32[2048]{0:T(1024)S(1)}, f32[2048]{0:T(1024)}, u32[]{:S(2)}) copy-start(f32[2048]{0:T(1024)} %param.22) | copy-start | bytes 24580
  66.6 10.8 %copy-start.10 = (f32[768]{0:T(1024)S(1)}, f32[768]{0:T(1024)}, u32[]{:S(2)}) copy-start(f32[768]{0:T(1024)} %param.24) | copy-start | bytes 9220
  70.9 9.9 %copy-start.2 = (f32[192,768]{1,0:T(8,128)S(1)}, f32[192,768]{1,0:T(8,128)}, u32[]{:S(2)}) copy-start(f32[192,768]{1,0:T(8,128)} %bitcast_multiply_fusion.1) | copy-start | bytes 1769476
  80.8 0.8 copy-start.4
  89.1 4.8 %collective-permute-start.2 = (bf16[12,1,32,4]{0,2,3,1:T(8,128)(2,1)S(1)}, bf16[12,1,32,4]{0,2,3,1:T(8,128)(2,1)S(1)}, u32[]{:S(2)}, u32[]{:S(2)}) collective-permute-start(bf16[12,1,32,4]{0,2,3,1:T(8,128)(2,1)S(1)} %get-tuple-element.44), channel_id=1, source_target_pairs={{0,8},{8,16},{16,24},{1,9},{9,17},{17,25},{2,10},{10,18},{18,26},{... | collective-permute-start | bytes 9224 | tf_op jit(solution)/shard_map/ppermute | solution.py:21
  91.2 3.1 %collective-permute-start.3 = (bf16[12,1,32,4]{0,2,3,1:T(8,128)(2,1)S(1)}, bf16[12,1,32,4]{0,2,3,1:T(8,128)(2,1)S(1)}, u32[]{:S(2)}, u32[]{:S(2)}) collective-permute-start(bf16[12,1,32,4]{0,2,3,1:T(8,128)(2,1)S(1)} %get-tuple-element.45), channel_id=1, source_target_pairs={{8,0},{16,8},{24,16},{9,1},{17,9},{25,17},{10,2},{18,10},{26,18},{... | collective-permute-start | bytes 9224 | tf_op jit(solution)/shard_map/ppermute | solution.py:24
Sparse Core Ops, SparseCore 0:
  9.6 37.6 all-gather.2
  48.8 28.5 all-gather.4
  129.8 123.2 all-reduce.6
where the time goes:
time: 265 us; the launch traced here: 263 us
  waiting for transfers between devices  89.9 us (34%)
  blocking collectives  67.9 us (26%)
  local copies, waits for them, and re-layouts  48.3 us (18%)
  matrix products  21.2 us (8%)
  between operations  14.1 us (5%)
  other arithmetic  12.5 us (5%)
  starting transfers between devices  8.67 us (3%)
    psum x1, waiting for transfers between devices, shards(): lax.psum((conv_part, gain_part, bias_part, embed_part), ('rows', 'batch'))  81.6 us
    psum x1, blocking collectives, shards(): lax.psum((conv_part, gain_part, bias_part, embed_part), ('rows', 'batch'))  40.5 us
    reshape x2, local copies, waits for them, and re-layouts, shards(): grouped = values.reshape(images, height * across, GROUPS, per_group)  14.3 us
    psum x1, blocking collectives, shards(): lax.psum((jnp.sum(grad_norm, axis=(1, 3)), jnp.sum(grad_norm * normed_gro...  12.4 us
    psum x1, blocking collectives, shards(): totals = lax.psum(jnp.sum(grouped, axis=(1, 3)), 'rows')  8.52 us
    unnamed x31, local copies, waits for them, and re-layouts  8.16 us
    mul x5, local copies, waits for them, and re-layouts, shards(): inverse * (grad_norm - (first / members)[:, None, :, None] - normed_group...  7.66 us
    sub x5, local copies, waits for them, and re-layouts, shards(): centred = grouped - (totals / members)[:, None, :, None]  7.65 us
  transfers between devices with their start and end apart: 7, of which 3 were waited for; matrix products, arithmetic and copies ran while one was open for 17% of the time, Pallas kernels for 0%

commit v1 on v0

v1 whole, which is shorter than its diff:
```python
import functools

import jax
import jax.numpy as jnp
from jax import lax
from jax.experimental import pallas as pl
from jax.experimental.pallas import tpu as pltpu
from jax.sharding import PartitionSpec as P

GROUPS = 32
LATENT = 4
PATCH = 2
EPS_NORM = 1e-06
EPS_UNIT = 1e-06
F32 = jnp.float32
BF16 = jnp.bfloat16
NT = (((1,), (1,)), ((), ()))
TN = (((0,), (0,)), ((), ()))


def dot(a, b, dims=(((1,), (0,)), ((), ()))):
    return lax.dot_general(a, b, dims, preferred_element_type=F32)


def split(x, parts):
    out = []
    for _ in range(parts):
        part = x.astype(BF16).astype(F32)
        out.append(part)
        x = x - part
    return out


def exact_dot(x, exact, parts, dims=(((1,), (0,)), ((), ()))):
    rows = x.shape[0]
    full = dot(jnp.concatenate(split(x, parts), axis=0).astype(BF16), exact, dims)
    return sum(full[i * rows : (i + 1) * rows] for i in range(parts))


def kernel(
    images, height, across, n,
    feat, gain, bias, taps, wslice, win, winb, wout, woutb, targ,
    out, conv_o, gb_o, emb_o,
    st, st_in, nrm, slope, act, gs_ref, halo, halo_in, ghalo, ghalo_in,
    vpart, v_in, vcat, pout, hact, hslope, gh_ref, a_ref, a_in, fs, fs_in, stat,
    s_send, s_recv, v_send, v_recv, x_send, x_recv, b_send, b_recv,
    h_send, h_recv, g_send, g_recv, a_send, a_recv, f_send, f_recv,
):
    me = lax.axis_index("rows")
    cells, channels = feat.shape
    area = height * across
    per_group = channels // GROUPS
    members = n * area * per_group
    hidden = win.shape[1]
    share = wout.shape[0]
    tokens = targ.shape[0]
    tok_cols = across // PATCH
    prev, following = lax.rem(me + n - 1, n), lax.rem(me + 1, n)
    sibling = me + 1 - 2 * lax.rem(me, 2)

    def send(src, dst, ss, rs, peer):
        return pltpu.make_async_remote_copy(
            src_ref=src, dst_ref=dst, send_sem=ss, recv_sem=rs,
            device_id={"rows": peer}, device_id_type=pl.DeviceIdType.MESH,
        )

    def spread(src, dst, ss, rs):
        return [
            send(src, dst.at[k - 1], ss.at[k - 1], rs.at[k - 1], lax.rem(me + k, n))
            for k in range(1, n)
        ]

    barrier = pltpu.get_barrier_semaphore()
    for k in range(1, n):
        pl.semaphore_signal(
            barrier, inc=1, device_id={"rows": lax.rem(me + k, n)},
            device_id_type=pl.DeviceIdType.MESH,
        )
    pl.semaphore_wait(barrier, n - 1)

    def slab(owner):
        return pout.at[pl.ds(pl.multiple_of(owner * share, share), share), :]

    own = pl.ds(pl.multiple_of(me * share, share), share)
    cross = [
        send(wout, slab(me), x_send.at[k - 1], x_recv.at[k - 1], lax.rem(me + 2 * k, n))
        for k in range(1, n // 2)
    ]
    beside = [send(wout, slab(me), b_send.at[0], b_recv.at[0], sibling)]
    for copy in cross + beside:
        copy.start()
    pout[own, :] = wout[...]

    st[...] = jnp.zeros_like(st)

    def stats(b, carry):
        x = feat[pl.ds(pl.multiple_of(b * area, area), area), :].astype(F32)
        total = jnp.sum(x, axis=0, keepdims=True)
        centred = x - total / area
        st[0, pl.ds(b, 1), :] = total
        st[1, pl.ds(b, 1), :] = jnp.sum(centred * centred, axis=0, keepdims=True)
        return carry

    lax.fori_loop(0, images, stats, 0)
    stat_copies = spread(st, st_in, s_send, s_recv)
    for copy in stat_copies:
        copy.start()

    vpart[...] = exact_dot(wslice[...], win[...], 2)
    v_copies = spread(vpart, v_in, v_send, v_recv)
    for copy in v_copies:
        copy.start()
    same = (
        lax.broadcasted_iota(jnp.int32, (channels, channels), 0) // per_group
        == lax.broadcasted_iota(jnp.int32, (channels, channels), 1) // per_group
    )
    pool = jnp.where(same, 1.0, 0.0).astype(BF16)

    for copy in stat_copies:
        copy.wait()
    sums = [st[0]] + [st_in[k, 0] for k in range(n - 1)]
    squares = [st[1]] + [st_in[k, 1] for k in range(n - 1)]
    mean = exact_dot(sum(sums), pool, 3) / members
    spread_sq = sum(
        sq + area * jnp.square(total / area - mean) for total, sq in zip(sums, squares)
    )
    variance = exact_dot(spread_sq, pool, 3) / members
    stat[0] = mean
    stat[1] = lax.rsqrt(variance + EPS_NORM)

    def forward(b, carry):
        where = pl.ds(pl.multiple_of(b * area, area), area)
        x = feat[where, :].astype(F32)
        normed = (x - stat[0, pl.ds(b, 1), :]) * stat[1, pl.ds(b, 1), :]
        shifted = normed * gain[...] + bias[...]
        sig = jax.nn.sigmoid(shifted)
        nrm[where, :] = normed
        act[where, :] = (shifted * sig).astype(BF16)
        slope[where, :] = sig * (1.0 + shifted * (1.0 - sig))
        return carry

    lax.fori_loop(0, images, forward, 0)

    lane = lax.broadcasted_iota(jnp.int32, (8, cells), 1)
    col = lax.rem(lane, across)
    row = lax.rem(lane // across, height)

    def ahead(x, count):
        return pltpu.roll(x, (-count) % cells, 1) if count % cells else x

    def beside_col(x, off):
        if off == 0:
            return x
        ok = (col + off >= 0) & (col + off < across)
        return jnp.where(ok, ahead(x, off), 0.0)

    def above(x, arrived):
        edge = jnp.where(me > 0, ahead(arrived, (height - 1) * across), 0.0)
        return jnp.where(row == 0, edge, ahead(x, -across))

    def below(x, arrived):
        edge = jnp.where(me < n - 1, ahead(arrived, -(height - 1) * across), 0.0)
        return jnp.where(row == height - 1, edge, ahead(x, across))

    terms = dot(taps[...], act[...], NT)
    rows3 = []
    for dy in range(3):
        rows3.append(
            sum(
                beside_col(terms[(3 * dy + dx) * 8 : (3 * dy + dx + 1) * 8], dx - 1)
                for dx in range(3)
            )
        )
    halo[0] = rows3[0]
    halo[1] = rows3[2]
    halo_copies = [
        send(halo.at[0], halo_in.at[0], h_send.at[0], h_recv.at[0], following),
        send(halo.at[1], halo_in.at[1], h_send.at[1], h_recv.at[1], prev),
    ]
    for copy in halo_copies:
        copy.start()
    cell = lax.broadcasted_iota(jnp.int32, (cells, tokens), 0)
    tok = lax.broadcasted_iota(jnp.int32, (cells, tokens), 1)
    per_image = (height // PATCH) * tok_cols
    corner = (
        (tok // per_image) * area
        + (lax.rem(tok, per_image) // tok_cols) * (PATCH * across)
        + lax.rem(tok, tok_cols) * PATCH
    )
    away = cell - corner
    pick = [
        jnp.where(away == u * across + v, 1.0, 0.0).astype(BF16)
        for u in range(PATCH) for v in range(PATCH)
    ]
    for copy in v_copies:
        copy.wait()
    v_all = vpart[...] + sum(v_in[k] for k in range(n - 1))
    inner = PATCH * PATCH * LATENT
    v_hi, v_lo = split(v_all[0:inner], 2)
    vcat[...] = jnp.concatenate([v_hi, v_hi, v_lo], axis=0).astype(BF16)
    pre_bias = v_all[inner : inner + 1] + winb[...]
    for copy in halo_copies:
        copy.wait()
    latent = rows3[1] + above(rows3[0], halo_in[0]) + below(rows3[2], halo_in[1])
    first_half = lax.broadcasted_iota(jnp.int32, (8, tokens), 0) < LATENT
    blocks = []
    for u in range(PATCH):
        pair = [exact_dot(latent, pick[u * PATCH + v], 3) for v in range(PATCH)]
        blocks.append(jnp.where(first_half, pair[0], pair[1]))
    patches = jnp.concatenate(blocks, axis=0)
    p_hi, p_lo = split(patches, 2)
    pcat = jnp.concatenate([p_hi, p_lo, p_hi], axis=0).astype(BF16)

    for copy in cross:
        copy.wait()
    relay = []
    for k in range(1, n // 2):
        owner = lax.rem(me + n - 2 * k, n)
        relay.append(send(slab(owner), slab(owner), b_send.at[k], b_recv.at[k], sibling))
    for copy in relay:
        copy.start()

    step = hidden // 4
    for c in range(4):
        where = slice(c * step, (c + 1) * step)
        pre = dot(pcat, vcat[:, where], TN) + pre_bias[:, where]
        sig = jax.nn.sigmoid(pre)
        hact[:, where] = (pre * sig).astype(BF16)
        hslope[:, where] = sig * (1.0 + pre * (1.0 - sig))
    target = targ[...].astype(F32)
    unit_target = target * lax.rsqrt(jnp.sum(target * target, axis=1, keepdims=True) + EPS_UNIT)
    for copy in beside + relay:
        copy.wait()
    projected = dot(hact[...], pout[...]) + woutb[...]
    inv_len = lax.rsqrt(jnp.sum(projected * projected, axis=1, keepdims=True) + EPS_UNIT)
    unit_proj = projected * inv_len
    cosine = jnp.sum(unit_proj * unit_target, axis=1, keepdims=True)
    grad_out = (-inv_len * (unit_target - cosine * unit_proj)).astype(BF16)
    for c in range(4):
        where = slice(c * step, (c + 1) * step)
        back = dot(grad_out, pout[where, :], NT)
        gh_ref[:, where] = (back * hslope[:, where]).astype(BF16)
    two = dot(vcat[inner:, :], gh_ref[...], NT)
    grad_patch = (two[0:inner] + two[inner:]).astype(BF16)

    grid = []
    for v in range(PATCH):
        grid.append(
            sum(
                dot(grad_patch[u * 8 : (u + 1) * 8], pick[u * PATCH + v], NT)
                for u in range(PATCH)
            )
        )
    low_rows = lax.broadcasted_iota(jnp.int32, (8, cells), 0) < LATENT
    both = jnp.where(low_rows, grid[0], grid[1])
    grad_lat = both + pltpu.roll(both, LATENT, 0)
    grad_lat = jnp.where(low_rows, grad_lat, 0.0)
    ghalo[...] = grad_lat
    ghalo_copies = [
        send(ghalo, ghalo_in.at[0], g_send.at[0], g_recv.at[0], following),
        send(ghalo, ghalo_in.at[1], g_send.at[1], g_recv.at[1], prev),
    ]
    for copy in ghalo_copies:
        copy.start()
    wide = dot(pcat[0 : 2 * inner], gh_ref[...])
    a_ref[...] = wide[0:inner] + wide[inner:]
    a_copies = spread(a_ref, a_in, a_send, a_recv)
    for copy in a_copies:
        copy.start()
    for copy in ghalo_copies:
        copy.wait()
    by_row = [below(grad_lat, ghalo_in[1]), grad_lat, above(grad_lat, ghalo_in[0])]
    grad_taps = jnp.concatenate(
        [beside_col(by_row[dy], 1 - dx) for dy in range(3) for dx in range(3)], axis=0
    ).astype(BF16)
    gs_ref[...] = dot(grad_taps, taps[...], TN)
    fs[...] = jnp.zeros_like(fs)

    def backward(b, carry):
        where = pl.ds(pl.multiple_of(b * area, area), area)
        gs = gs_ref[where, :] * slope[where, :]
        gs_ref[where, :] = gs
        fs[0, pl.ds(b, 1), :] = jnp.sum(gs, axis=0, keepdims=True)
        fs[1, pl.ds(b, 1), :] = jnp.sum(gs * nrm[where, :], axis=0, keepdims=True)
        return carry

    lax.fori_loop(0, images, backward, 0)
    f_copies = spread(fs, fs_in, f_send, f_recv)
    for copy in f_copies:
        copy.start()
    gb_o[0:1, :] = jnp.sum(fs[1], axis=0, keepdims=True)
    gb_o[1:2, :] = jnp.sum(fs[0], axis=0, keepdims=True)
    gb_o[2:8, :] = jnp.zeros((6, channels), F32)
    conv_o[...] = dot(grad_taps, act[...])
    for copy in a_copies:
        copy.wait()
    a_all = a_ref[...] + sum(a_in[k] for k in range(n - 1))
    emb_o[...] = exact_dot(a_all, win[...], 2, NT)
    for copy in f_copies:
        copy.wait()
    for i in range(2):
        total = (fs[i] + sum(fs_in[k, i] for k in range(n - 1))) * gain[...]
        stat_i = exact_dot(total, pool, 3) / members
        stat[2 + i] = stat_i

    def finish(b, carry):
        where = pl.ds(pl.multiple_of(b * area, area), area)
        one = pl.ds(b, 1)
        out[where, :] = (
            stat[1, one, :]
            * (gs_ref[where, :] * gain[...] - stat[2, one, :] - nrm[where, :] * stat[3, one, :])
        ).astype(BF16)
        return carry

    lax.fori_loop(0, images, finish, 0)


def shards(
    features, norm_gain, norm_bias, conv_weight, embed_weight, embed_bias,
    proj_in, proj_in_bias, proj_out, proj_out_bias, targets,
):
    images, height, across, channels = features.shape
    n = lax.axis_size("rows")
    me = lax.axis_index("rows")
    cells = images * height * across
    align = targets.shape[-1]
    tokens = targets.shape[0] * targets.shape[1] * targets.shape[2]
    inner, width = embed_weight.shape
    part, hidden = proj_in.shape
    share = proj_out.shape[0]
    pad_images = -(-images // 8) * 8
    taps = conv_weight.reshape(LATENT, 9, channels).transpose(1, 0, 2)
    taps = jnp.concatenate([taps, taps], axis=1).reshape(72, channels)
    wide = jnp.concatenate(
        [embed_weight, embed_bias[None], jnp.zeros((7, width), F32)], axis=0
    )
    wslice = lax.dynamic_slice_in_dim(wide, me * part, part, axis=1)
    rows = wslice.shape[0]
    dma = pltpu.SemaphoreType.DMA
    chips = max(n // 2 - 1, 1)
    vm = pltpu.VMEM
    grad_features, conv, gb, emb = pl.pallas_call(
        functools.partial(kernel, images, height, across, n),
        out_shape=(
            jax.ShapeDtypeStruct((cells, channels), BF16),
            jax.ShapeDtypeStruct((72, channels), F32),
            jax.ShapeDtypeStruct((8, channels), F32),
            jax.ShapeDtypeStruct((inner, part), F32),
        ),
        in_specs=[pl.BlockSpec(memory_space=vm)] * 10,
        out_specs=[pl.BlockSpec(memory_space=vm)] * 4,
        scratch_shapes=[
            vm((2, pad_images, channels), F32),
            vm((n - 1, 2, pad_images, channels), F32),
            vm((cells, channels), F32),
            vm((cells, channels), F32),
            vm((cells, channels), BF16),
            vm((cells, channels), F32),
            vm((2, 8, cells), F32),
            vm((2, 8, cells), F32),
            vm((8, cells), F32),
            vm((2, 8, cells), F32),
            vm((rows, hidden), F32),
            vm((n - 1, rows, hidden), F32),
            vm((3 * inner, hidden), BF16),
            vm((n * share, align), BF16),
            vm((tokens, hidden), BF16),
            vm((tokens, hidden), F32),
            vm((tokens, hidden), BF16),
            vm((inner, hidden), F32),
            vm((n - 1, inner, hidden), F32),
            vm((2, pad_images, channels), F32),
            vm((n - 1, 2, pad_images, channels), F32),
            vm((4, pad_images, channels), F32),
            dma((n - 1,)), dma((n - 1,)), dma((n - 1,)), dma((n - 1,)),
            dma((chips,)), dma((chips,)), dma((chips + 1,)), dma((chips + 1,)),
            dma((2,)), dma((2,)), dma((2,)), dma((2,)),
            dma((n - 1,)), dma((n - 1,)), dma((n - 1,)), dma((n - 1,)),
        ],
        compiler_params=pltpu.CompilerParams(
            collective_id=0, has_side_effects=True, vmem_limit_bytes=60 * 1024 * 1024
        ),
        name="alignment_step",
    )(
        features.reshape(cells, channels), norm_gain[None], norm_bias[None], taps, wslice,
        proj_in, proj_in_bias[None], proj_out, proj_out_bias[None],
        targets.reshape(tokens, align),
    )
    embed_part = lax.dynamic_update_slice_in_dim(
        jnp.zeros((inner, width), F32), emb, me * part, axis=1
    )
    conv, gb, grad_embed = lax.psum((conv, gb, embed_part), ("rows", "batch"))
    grad_conv = (
        conv.reshape(9, 8, channels)[:, :LATENT].transpose(1, 0, 2).reshape(LATENT, 9 * channels)
    )
    return (
        grad_features.reshape(images, height, across, channels),
        grad_conv, gb[0], gb[1], grad_embed,
    )


def solution(mesh):
    in_specs = (
        P("batch", "rows", None, None), P(), P(), P(), P(), P(),
        P("rows", None), P(), P("rows", None), P(), P("batch", "rows", None, None),
    )
    out_specs = (P("batch", "rows", None, None), P(), P(), P(), P())
    return jax.shard_map(shards, mesh=mesh, in_specs=in_specs, out_specs=out_specs, check_vma=False)
```

time: 265 us -> 206 us (0.78)
  Pallas kernels: 0 us -> 53.3 us
  local copies, waits for them, and re-layouts: 48.3 us -> 9.65 us
  blocking collectives: 67.9 us -> 39.8 us
  matrix products: 21.2 us -> 0 us
  other arithmetic: 12.5 us -> 0.69 us
  starting transfers between devices: 8.67 us -> 0.04 us
    pallas_call x0 -> x1, Pallas kernels: none -> 53.3 us  [shards(): pl.pallas_call(functools.partial(kernel, images, height, across, n), out_...]
    psum x4 -> x1, blocking collectives: 67.9 us -> 39.8 us  [shards(): conv, gb, grad_embed = lax.psum((conv, gb, embed_part), ('rows', 'batch'))]
    dot_general x9 -> x0, matrix products: 21.2 us -> none  [the longest x1 6.39 us: shards(): lax.dot_general(grad_hidden, full_in, (((1,), (1,)), ((), ())), preferred...]
    reshape x7 -> x2, local copies, waits for them, and re-layouts: 18.5 us -> 2.57 us  [the longest x1 1.78 us: shards(): conv.reshape(9, 8, channels)[:, :LATENT].transpose(1, 0, 2)]
    mul x8 -> x0, local copies, waits for them, and re-layouts: 9.56 us -> none  [the longest x5 7.66 us: shards(): inverse * (grad_norm - (first / members)[:, None, :, None] - normed_group...]
    ppermute x4 -> x0, starting transfers between devices: 8.56 us -> none  [the longest x2 5.77 us: padded(): lax.ppermute(lax.slice_in_dim(block, block.shape[dim] - width, None, axis...]
    sub x7 -> x0, local copies, waits for them, and re-layouts: 7.89 us -> none  [the longest x5 7.65 us: shards(): centred = grouped - (totals / members)[:, None, :, None]]
    all_gather x2 -> x0, waiting for transfers between devices: 6.48 us -> none  [the longest x1 6.45 us: shards(): lax.all_gather(proj_out, 'rows', axis=0, tiled=True)]
  transfers between devices with their start and end apart: 7 -> 1, of which waited for: 3 -> 1; matrix products, arithmetic and copies ran while one was open for 17% -> 0% of each run, Pallas kernels for 0% -> 0%
where the time goes in v1:
time: 206 us; the launch traced here: 205 us
  waiting for transfers between devices  87.6 us (43%)
  Pallas kernels  53.3 us (26%)
  blocking collectives  39.8 us (19%)
  between operations  14.1 us (7%)
  local copies, waits for them, and re-layouts  9.65 us (5%)
    psum x1, waiting for transfers between devices, shards(): conv, gb, grad_embed = lax.psum((conv, gb, embed_part), ('rows', 'batch'))  87.6 us
    pallas_call x1, Pallas kernels, shards(): pl.pallas_call(functools.partial(kernel, images, height, across, n), out_...  53.3 us
    psum x1, blocking collectives, shards(): conv, gb, grad_embed = lax.psum((conv, gb, embed_part), ('rows', 'batch'))  39.8 us
    unnamed x18, local copies, waits for them, and re-layouts  4.42 us
  transfers between devices with their start and end apart: 1, of which 1 were waited for; matrix products, arithmetic and copies ran while one was open for 0% of the time, Pallas kernels for 0%

profile of v1, /device:TPU:0, one launch (start us, length us, event | category | flops | bytes accessed | tf_op | source)
XLA Modules:
  0.0 205.1 jit_solution(4082367136816547457)
XLA Ops:
  7.2 0.0 all-reduce.3.cloned.1.call-start
  7.2 0.8 reshape.32
  8.0 0.0 copy-start.6
  8.0 0.0 copy-start.2
  8.1 0.7 copy.22
  8.7 0.0 copy-done.6
  8.7 0.6 broadcast_in_dim.26.woutb
  9.3 0.1 pad.2.clone
  9.4 0.0 copy-done.2
  9.4 0.6 copy-done.5
  10.0 0.7 fusion.1.wslice
  10.7 53.3 %alignment_step.1 = (bf16[768,512]{1,0:T(8,128)(2,1)}, f32[72,512]{1,0:T(8,128)}, f32[8,512]{1,0:T(8,128)}, f32[16,256]{1,0:T(8,128)}) custom-call(bf16[768,512]{1,0:T(8,128)(2,1)} %bitcast.19, f32[1,512]{1,0:T(1,128)} %bitcast.27, f32[1,512]{1,0:T(1,128)} %bitcast.28, bf16[72,512]{1,0:T(8,128)(2,1)} %bitcast.21, f32[24,256]{1,0:T(8,128)} %fusion.1.wslice, ...), custom_call_target="tpu_custom_call" | custom-call | tf_op jit(solution)/shard_map/alignment_step/pallas_call | solution.py:342
  64.0 1.8 copy.19
  65.8 0.7 constant_dynamic-update-slice_fusion
  66.5 0.6 copy-done.1
  67.1 0.0 all-reduce.3.cloned.1.call-update
  67.1 0.1 copy-done.4
  67.2 39.8 %psum.22 = f32[8,512]{1,0:T(8,128)S(1)} all-reduce(f32[8,512]{1,0:T(8,128)S(1)} %copy-done.4), channel_id=1, replica_groups=mesh['rows'=4,'batch'=8] {'rows','batch'}, use_global_device_ids=true, to_apply=%region_1.0 | all-reduce | flops 4096 | bytes 32768 | tf_op jit(solution)/shard_map/psum | solution.py:392
  107.0 0.6 fusion.2
  107.6 87.6 %all-reduce.3.cloned.1.call-done = (f32[9,8,512]{2,0,1:T(8,128)}, f32[16,1024]{1,0:T(8,128)}) async-done(((f32[9,8,512]{2,0,1:T(8,128)}, f32[16,1024]{1,0:T(8,128)}), (f32[9,8,512]{2,0,1:T(8,128)}, f32[16,1024]{1,0:T(8,128)})) %all-reduce.3.cloned.1.call-update) | async-done | bytes 213008 | tf_op jit(solution)/shard_map/psum | solution.py:392
  195.2 0.9 slice_bitcast_fusion
  196.1 0.7 copy.20
  196.8 0.9 copy.27
  197.7 0.6 copy.28
  (10 shorter events, 0.0 us)
Async XLA Ops:
  7.2 188.0 %all-reduce.3.cloned.1.call-start = ((), (), s32[]{:S(2)}) async-start(), calls=%async_computation | async-start | bytes 655360 | tf_op jit(solution)/shard_map/psum | solution.py:392
  8.0 0.7 copy-start.6
  8.0 1.4 copy-start.2
  9.3 0.7 copy-start.5
  64.0 132.8 %copy-start = (bf16[768,512]{1,0:T(8,128)(2,1)S(1)}, bf16[768,512]{1,0:T(8,128)(2,1)}, u32[]{:S(2)}) copy-start(bf16[768,512]{1,0:T(8,128)(2,1)} %get-tuple-element.9) | copy-start | bytes 2359300
  66.5 0.6 copy-start.1
  66.5 0.7 copy-start.4
  196.8 0.9 copy-start.3
Sparse Core Ops, SparseCore 0:
  67.3 127.8 all-reduce.2

commit v2 on v1

--- a/solution.py
+++ b/solution.py
@@ -38,13 +38,15 @@
 
 
 def kernel(
-    images, height, across, n,
+    images, height, across, n, nb,
     feat, gain, bias, taps, wslice, win, winb, wout, woutb, targ,
-    out, conv_o, gb_o, emb_o,
+    out, conv_o, gain_o, bias_o, emb_o,
     st, st_in, nrm, slope, act, gs_ref, halo, halo_in, ghalo, ghalo_in,
     vpart, v_in, vcat, pout, hact, hslope, gh_ref, a_ref, a_in, fs, fs_in, stat,
+    pack, pack_in, piece, piece_in, emb, emb_in, whole, whole_emb,
     s_send, s_recv, v_send, v_recv, x_send, x_recv, b_send, b_recv,
     h_send, h_recv, g_send, g_recv, a_send, a_recv, f_send, f_recv,
+    p_send, p_recv, q_send, q_recv, e_send, e_recv, w_send, w_recv, y_send, y_recv,
 ):
     me = lax.axis_index("rows")
     cells, channels = feat.shape
@@ -76,7 +78,13 @@
             barrier, inc=1, device_id={"rows": lax.rem(me + k, n)},
             device_id_type=pl.DeviceIdType.MESH,
         )
-    pl.semaphore_wait(barrier, n - 1)
+    group = lax.axis_index("batch")
+    for k in range(1, nb):
+        pl.semaphore_signal(
+            barrier, inc=1, device_id={"batch": lax.rem(group + k, nb)},
+            device_id_type=pl.DeviceIdType.MESH,
+        )
+    pl.semaphore_wait(barrier, n + nb - 2)
 
     def slab(owner):
         return pout.at[pl.ds(pl.multiple_of(owner * share, share), share), :]
@@ -288,14 +296,57 @@
     f_copies = spread(fs, fs_in, f_send, f_recv)
     for copy in f_copies:
         copy.start()
-    gb_o[0:1, :] = jnp.sum(fs[1], axis=0, keepdims=True)
-    gb_o[1:2, :] = jnp.sum(fs[0], axis=0, keepdims=True)
-    gb_o[2:8, :] = jnp.zeros((6, channels), F32)
-    conv_o[...] = dot(grad_taps, act[...])
+    conv = dot(grad_taps, act[...])
+    gain_row = jnp.sum(fs[1], axis=0, keepdims=True)
+    bias_row = jnp.sum(fs[0], axis=0, keepdims=True)
+    row8 = lax.broadcasted_iota(jnp.int32, (8, channels), 0)
+    per = pack.shape[1] // 8
+    lanes = pack.shape[2]
+    for i in range(5):
+        block = conv[16 * i : 16 * i + 8]
+        if i < 4:
+            block = block + pltpu.roll(conv[16 * i + 8 : 16 * i + 16], LATENT, 0)
+        else:
+            block = jnp.where(row8 == LATENT, gain_row, block)
+            block = jnp.where(row8 == LATENT + 1, bias_row, block)
+        for c in range(channels // lanes):
+            t = 5 * c + i
+            pack[t // per, (t % per) * 8 : (t % per + 1) * 8, :] = (
+                block[:, c * lanes : (c + 1) * lanes]
+            )
+    for t in range(5 * (channels // lanes), n * per):
+        pack[t // per, (t % per) * 8 : (t % per + 1) * 8, :] = jnp.zeros((8, lanes), F32)
+    p_copies = []
+    for k in range(1, n):
+        peer = lax.rem(me + k, n)
+        p_copies.append(
+            send(pack.at[peer], pack_in.at[k - 1], p_send.at[k - 1], p_recv.at[k - 1], peer)
+        )
+    for copy in p_copies:
+        copy.start()
     for copy in a_copies:
         copy.wait()
     a_all = a_ref[...] + sum(a_in[k] for k in range(n - 1))
-    emb_o[...] = exact_dot(a_all, win[...], 2, NT)
+    emb[...] = exact_dot(a_all, win[...], 2, NT)
+
+    def across_batch(src, dst, ss, rs):
+        return [
+            pltpu.make_async_remote_copy(
+                src_ref=src, dst_ref=dst.at[k - 1], send_sem=ss.at[k - 1], recv_sem=rs.at[k - 1],
+                device_id={"batch": lax.rem(group + k, nb)}, device_id_type=pl.DeviceIdType.MESH,
+            )
+            for k in range(1, nb)
+        ]
+
+    q_copies = across_batch(emb, emb_in, e_send, e_recv)
+    for copy in q_copies:
+        copy.start()
+    for copy in p_copies:
+        copy.wait()
+    piece[...] = pack[me] + sum(pack_in[k] for k in range(n - 1))
+    piece_copies = across_batch(piece, piece_in, q_send, q_recv)
+    for copy in piece_copies:
+        copy.start()
     for copy in f_copies:
         copy.wait()
     for i in range(2):
@@ -312,7 +363,50 @@
         ).astype(BF16)
         return carry
 
-    lax.fori_loop(0, images, finish, 0)
+    lax.fori_loop(0, images // 2, finish, 0)
+    for copy in q_copies + piece_copies:
+        copy.wait()
+    whole[me] = ordered(piece, piece_in, group, nb)
+    whole_emb[me] = ordered(emb, emb_in, group, nb)
+    w_copies = []
+    for k in range(1, n):
+        peer = lax.rem(me + k, n)
+        w_copies.append(send(whole.at[me], whole.at[me], w_send.at[k - 1], w_recv.at[k - 1], peer))
+        w_copies.append(
+            send(whole_emb.at[me], whole_emb.at[me], y_send.at[k - 1], y_recv.at[k - 1], peer)
+        )
+    for copy in w_copies:
+        copy.start()
+    lax.fori_loop(images // 2, images, finish, 0)
+    for copy in w_copies:
+        copy.wait()
+    for c in range(channels // lanes):
+        at = slice(c * lanes, (c + 1) * lanes)
+        for i in range(5):
+            t = 5 * c + i
+            tile = whole[t // per, (t % per) * 8 : (t % per + 1) * 8, :]
+            for half in range(2):
+                tap = 2 * i + half
+                rows = tile[half * LATENT : (half + 1) * LATENT]
+                if tap < 9:
+                    start = tap * channels + c * lanes
+                    conv_o[:, start : start + lanes] = rows
+                else:
+                    gain_o[:, at] = rows[0:1]
+                    bias_o[:, at] = rows[1:2]
+    part = emb.shape[1]
+    for k in range(n):
+        emb_o[:, k * part : (k + 1) * part] = whole_emb[k]
+
+
+def ordered(own, arrived, group, nb):
+    total = None
+    for g in range(nb):
+        slot = lax.rem(group + nb - g, nb)
+        value = arrived[jnp.maximum(slot - 1, 0)] if nb > 1 else own[...]
+        value = jnp.where(slot == 0, own[...], value)
+        total = value if total is None else total + value
+    return total
 
 
 def shards(
@@ -321,6 +415,9 @@
 ):
     images, height, across, channels = features.shape
     n = lax.axis_size("rows")
+    nb = lax.axis_size("batch")
+    lanes = 128
+    per = -(-(5 * (channels // lanes)) // n)
     me = lax.axis_index("rows")
     cells = images * height * across
     align = targets.shape[-1]
@@ -339,16 +436,17 @@
     dma = pltpu.SemaphoreType.DMA
     chips = max(n // 2 - 1, 1)
     vm = pltpu.VMEM
-    grad_features, conv, gb, emb = pl.pallas_call(
-        functools.partial(kernel, images, height, across, n),
+    grad_features, grad_conv, grad_gain, grad_bias, grad_embed = pl.pallas_call(
+        functools.partial(kernel, images, height, across, n, nb),
         out_shape=(
             jax.ShapeDtypeStruct((cells, channels), BF16),
-            jax.ShapeDtypeStruct((72, channels), F32),
-            jax.ShapeDtypeStruct((8, channels), F32),
-            jax.ShapeDtypeStruct((inner, part), F32),
+            jax.ShapeDtypeStruct((LATENT, 9 * channels), F32),
+            jax.ShapeDtypeStruct((1, channels), F32),
+            jax.ShapeDtypeStruct((1, channels), F32),
+            jax.ShapeDtypeStruct((inner, width), F32),
         ),
         in_specs=[pl.BlockSpec(memory_space=vm)] * 10,
-        out_specs=[pl.BlockSpec(memory_space=vm)] * 4,
+        out_specs=[pl.BlockSpec(memory_space=vm)] * 5,
         scratch_shapes=[
             vm((2, pad_images, channels), F32),
             vm((n - 1, 2, pad_images, channels), F32),
@@ -372,9 +470,21 @@
             vm((2, pad_images, channels), F32),
             vm((n - 1, 2, pad_images, channels), F32),
             vm((4, pad_images, channels), F32),
+            vm((n, per * 8, lanes), F32),
+            vm((n - 1, per * 8, lanes), F32),
+            vm((per * 8, lanes), F32),
+            vm((max(nb - 1, 1), per * 8, lanes), F32),
+            vm((inner, part), F32),
+            vm((max(nb - 1, 1), inner, part), F32),
+            vm((n, per * 8, lanes), F32),
+            vm((n, inner, part), F32),
             dma((n - 1,)), dma((n - 1,)), dma((n - 1,)), dma((n - 1,)),
             dma((chips,)), dma((chips,)), dma((chips + 1,)), dma((chips + 1,)),
             dma((2,)), dma((2,)), dma((2,)), dma((2,)),
+            dma((n - 1,)), dma((n - 1,)), dma((n - 1,)), dma((n - 1,)),
+            dma((n - 1,)), dma((n - 1,)),
+            dma((max(nb - 1, 1),)), dma((max(nb - 1, 1),)),
+            dma((max(nb - 1, 1),)), dma((max(nb - 1, 1),)),
             dma((n - 1,)), dma((n - 1,)), dma((n - 1,)), dma((n - 1,)),
         ],
         compiler_params=pltpu.CompilerParams(
@@ -386,16 +496,9 @@
         proj_in, proj_in_bias[None], proj_out, proj_out_bias[None],
         targets.reshape(tokens, align),
     )
-    embed_part = lax.dynamic_update_slice_in_dim(
-        jnp.zeros((inner, width), F32), emb, me * part, axis=1
-    )
-    conv, gb, grad_embed = lax.psum((conv, gb, embed_part), ("rows", "batch"))
-    grad_conv = (
-        conv.reshape(9, 8, channels)[:, :LATENT].transpose(1, 0, 2).reshape(LATENT, 9 * channels)
-    )
     return (
         grad_features.reshape(images, height, across, channels),
-        grad_conv, gb[0], gb[1], grad_embed,
+        grad_conv, grad_gain[0], grad_bias[0], grad_embed,
     )
 
 

time: 206 us -> 73.7 us (0.36)
  waiting for transfers between devices: 87.6 us -> 0 us
  blocking collectives: 39.8 us -> 0 us
  between operations: 14.1 us -> 0.7 us
  Pallas kernels: 53.3 us -> 64.6 us
  local copies, waits for them, and re-layouts: 9.65 us -> 6.62 us
    psum x1 -> x0, waiting for transfers between devices: 87.6 us -> none  [shards(): conv, gb, grad_embed = lax.psum((conv, gb, embed_part), ('rows', 'batch'))]
    psum x1 -> x0, blocking collectives: 39.8 us -> none  [shards(): conv, gb, grad_embed = lax.psum((conv, gb, embed_part), ('rows', 'batch'))]
    pallas_call x1, Pallas kernels: 53.3 us -> 64.6 us  [shards(): pl.pallas_call(functools.partial(kernel, images, height, across, n, nb),...]
    unnamed x18 -> x19, local copies, waits for them, and re-layouts: 4.42 us -> 5.26 us
  transfers between devices with their start and end apart: 1 -> 0, of which waited for: 1 -> 0; matrix products, arithmetic and copies ran while one was open for 0% -> 0% of each run, Pallas kernels for 0% -> 0%
where the time goes in v2:
time: 73.7 us; the launch traced here: 73.4 us
  Pallas kernels  64.6 us (88%)
  local copies, waits for them, and re-layouts  6.62 us (9%)
  other arithmetic  1.42 us (2%)
    pallas_call x1, Pallas kernels, shards(): pl.pallas_call(functools.partial(kernel, images, height, across, n, nb),...  64.6 us
    unnamed x19, local copies, waits for them, and re-layouts  5.26 us

profile of v2, /device:TPU:0, one launch (start us, length us, event | category | flops | bytes accessed | tf_op | source)
XLA Modules:
  0.0 73.4 jit_solution(2340195772735616786)
XLA Ops:
  0.6 0.0 copy-start.4
  0.7 0.0 copy-start.3
  0.7 0.1 pad.2.clone
  0.7 0.6 copy-done.4
  1.3 0.6 broadcast_in_dim.23.woutb
  1.9 0.0 copy-done.3
  1.9 0.0 copy-start.2
  1.9 1.4 %fusion.1.wslice = f32[24,256]{1,0:T(8,128)} fusion(s32[]{:T(128)S(6)} %select_n.3, f32[16,1024]{1,0:T(8,128)} %param.15, f32[1,1024]{1,0:T(1,128)S(1)} %bitcast.19, f32[24]{0:T(128)S(1)} %pad.2.clone), kind=kLoop, calls=%fused_computation.5 | loop fusion | flops 12288 | bytes 94308 | tf_op jit(solution)/shard_map/concatenate | solution.py:431
  3.3 0.0 copy-done.2
  3.4 0.7 copy.19
  4.0 64.6 %alignment_step.1 = (bf16[768,512]{1,0:T(8,128)(2,1)}, f32[4,4608]{1,0:T(4,128)}, f32[1,512]{1,0:T(1,128)}, f32[1,512]{1,0:T(1,128)}, f32[16,1024]{1,0:T(8,128)}) custom-call(bf16[768,512]{1,0:T(8,128)(2,1)} %bitcast.14, f32[1,512]{1,0:T(1,128)} %bitcast.20, f32[1,512]{1,0:T(1,128)} %bitcast.21, bf16[72,512]{1,0:T(8,128)(2,1)} %bitcast.16, ...), custom_call_target="tpu_custom_call" | custom-call | tf_op jit(solution)/shard_map/alignment_step/pallas_call | solution.py:439
  68.7 0.0 copy-start
  68.7 2.1 %copy.25 = bf16[12,2,32,512]{3,2,1,0:T(8,128)(2,1)} copy(bf16[12,2,32,512]{3,2,1,0:T(8,128)(2,1)} %bitcast.13) | data formatting | bytes 1572864
  70.8 0.0 copy-done
  70.8 0.0 copy-start.6
  70.8 0.0 copy-start.1
  70.8 0.6 copy.26
  71.5 0.0 copy-done.6
  71.5 0.0 copy-start.5
  71.5 0.6 copy.27
  72.1 0.1 copy-done.5
  72.2 0.6 copy.28
  72.7 0.0 copy-done.1
  72.7 0.6 copy.29
  (3 shorter events, 0.0 us)
Async XLA Ops:
  0.6 0.7 copy-start.4
  0.7 1.3 %copy-start.3 = (f32[1024]{0:T(1024)S(1)}, f32[1024]{0:T(1024)}, u32[]{:S(2)}) copy-start(f32[1024]{0:T(1024)} %param.16) | copy-start | bytes 12292
  1.9 1.4 %copy-start.2 = (bf16[4,4608]{1,0:T(4,128)(2,1)S(1)}, bf16[4,4608]{1,0:T(4,128)(2,1)}, u32[]{:S(2)}) copy-start(bf16[4,4608]{1,0:T(4,128)(2,1)} %param.14) | copy-start | bytes 110596
  68.7 2.1 %copy-start = (f32[4,4608]{1,0:T(4,128)S(1)}, f32[4,4608]{1,0:T(4,128)}, u32[]{:S(2)}) copy-start(f32[4,4608]{1,0:T(4,128)} %get-tuple-element.21) | copy-start | bytes 221188
  70.8 0.7 copy-start.6
  70.8 1.9 %copy-start.1 = (f32[16,1024]{1,0:T(8,128)S(1)}, f32[16,1024]{1,0:T(8,128)}, u32[]{:S(2)}) copy-start(f32[16,1024]{1,0:T(8,128)} %get-tuple-element.24) | copy-start | bytes 196612
  71.5 0.7 copy-start.5
